TPU v7x, 256 devices: a whole 4x4x8 slice. The times are simulated.
256 devices in a mesh: ep: 16 (over y, x), fsdp: 16 (over z, core).
Axes of the slice: x: 4, y: 4, z: 8, core: 2. Of those that a mesh axis runs over, the one named last changes fastest.
Arguments:
- w_gate: float32 [64, 2048, 1024], P('ep', 'fsdp'), may hold values from -0.1875 to 0.1875
- avg_gate: bfloat16 [64, 2048, 1024], P('ep', 'fsdp'), may hold values from -0.0625 to 0.0625
- w_up: float32 [64, 2048, 1024], P('ep', 'fsdp'), may hold values from -0.1875 to 0.1875
- avg_up: bfloat16 [64, 2048, 1024], P('ep', 'fsdp'), may hold values from -0.0625 to 0.0625
- w_down: float32 [64, 1024, 2048], P('ep', None, 'fsdp'), may hold values from -0.25 to 0.25
- avg_down: bfloat16 [64, 1024, 2048], P('ep', None, 'fsdp'), may hold values from -0.09375 to 0.09375
- router_weight: float32 [2048, 64], P('fsdp', 'ep'), may hold values from -0.125 to 0.125
- router_gain: float32 [2048], P('fsdp'), may hold values from 0.25 to 1.75
Outputs:
- serve_gate: bfloat16 [64, 2048, 1024], P('ep', None, 'fsdp')
- serve_up: bfloat16 [64, 2048, 1024], P('ep', None, 'fsdp')
- serve_down: bfloat16 [64, 1024, 2048], P('ep', 'fsdp')
- scale_gate: float32 [64, 1024], P('ep', 'fsdp')
- scale_up: float32 [64, 1024], P('ep', 'fsdp')
- scale_down: float32 [64, 1024], P('ep', 'fsdp')
- serve_router: bfloat16 [2048, 64], replicated
All inputs are finite; a program needn't handle non-finite values.
Results may differ from a plain program's by a relative error of at most 0.001.
Values may be sent and summed in bfloat16 or wider, within the bound.
No kernel may reach another device: no remote copies, remote signals or barrier semaphores. Data moves between devices by JAX's collectives and lax.ppermute only.
A program may use at most 64 MiB of HBM per device.

v0:
```python
import jax
import jax.numpy as jnp
from jax import lax
from jax.experimental import pallas as pl
from jax.experimental.pallas import tpu as pltpu
from jax.sharding import PartitionSpec as P


CHIPS = 8
POWER = 17.0
LIFT = 2.0 ** (126.0 / 17.0)
TINY = 1e-37
F32, BF16 = jnp.float32, jnp.bfloat16

PARTNERS = (
    (4, 0), (4, 1), (3, 0), (5, 0), (1, 0), (7, 0), (1, 1), (7, 1),
    (2, 0), (6, 0), (0, 1), (2, 1), (6, 1), (3, 1), (5, 1),
)
FIRST = 4
REST = (3, 5, 2, 6, 0, 1, 7)
STAGES = (12, 14, 16)
AHEAD = 8


def position():
    me = lax.axis_index("fsdp")
    return lax.shift_right_logical(me, 1), lax.bitwise_and(me, 1)


def power(x):
    x2 = x * x
    x4 = x2 * x2
    x8 = x4 * x4
    return x8 * x8 * x


def normalised(fresh, axis):
    total = jnp.sum(fresh * fresh, axis=axis, keepdims=True)
    y = power(fresh * (lax.rsqrt(jnp.maximum(total, TINY)) * LIFT))
    return total, y.astype(BF16)


def send_off(out_buf, pieces, sem, i, part, parts, stores):
    _, core = position()
    size = 768 // parts
    at = pl.ds(part * size, size)
    for flip in range(2):
        copy = pltpu.make_async_copy(
            out_buf.at[2 * i + lax.bitwise_xor(core, flip), at],
            pieces[2 * i + flip].at[at],
            sem.at[2 * i + flip, part],
        )
        copy.start()
        stores.append(copy)


def first_kernel(wg, ag, wu, au, wd, ad, piece_0, piece_1, sums_out, *scratch):
    *bufs, out_buf, sums, sem, out_sem, sums_sem = scratch
    chip, _ = position()
    at = pl.ds(pl.multiple_of(lax.rem(chip + FIRST, CHIPS) * 128, 128), 128)
    views = [r.at[:, :, at] for r in (wg, ag, wu, au)]
    views += [r.at[:, at, :] for r in (wd, ad)]
    copies = [
        pltpu.make_async_copy(v, b, sem.at[n]) for n, (v, b) in enumerate(zip(views, bufs))
    ]
    for c in copies:
        c.start()
    lane = lax.broadcasted_iota(jnp.int32, (128, 128), 1)
    tall = jnp.zeros((128, 128), F32)
    stores = []
    for a in range(3):
        copies[2 * a].wait()
        copies[2 * a + 1].wait()
        for e in range(4):
            q = a * 4 + e
            fresh = bufs[2 * a][e] + bufs[2 * a + 1][e].astype(F32)
            total, y = normalised(fresh, 0 if a < 2 else 1)
            if a < 2:
                sums[q : q + 1, :] = total
                y = y.T
            else:
                tall = jnp.where(lane == e, total, tall)
            out_buf[0, q * 64 : q * 64 + 64, :] = y[:64]
            out_buf[1, q * 64 : q * 64 + 64, :] = y[64:]
        send_off(out_buf, (piece_0, piece_1), out_sem, 0, a, 3, stores)
    sums[8:16, :] = tall.T[0:8]
    copy = pltpu.make_async_copy(sums, sums_out, sums_sem)
    copy.start()
    for c in (*stores, copy):
        c.wait()


def encode_first(arrays):
    anywhere = pl.BlockSpec(memory_space=pl.ANY)
    return pl.pallas_call(
        first_kernel,
        in_specs=[anywhere] * 6,
        out_specs=[anywhere] * 3,
        out_shape=[jax.ShapeDtypeStruct((768, 128), BF16)] * 2
        + [jax.ShapeDtypeStruct((16, 128), F32)],
        scratch_shapes=[pltpu.VMEM((4, 128, 128), t) for t in (F32, BF16) * 3]
        + [
            pltpu.VMEM((2, 768, 128), BF16),
            pltpu.VMEM((16, 128), F32),
            pltpu.SemaphoreType.DMA((6,)),
            pltpu.SemaphoreType.DMA((2, 3)),
            pltpu.SemaphoreType.DMA,
        ],
        cost_estimate=pl.CostEstimate(
            flops=2_500_000, bytes_accessed=1_600_000, transcendentals=0
        ),
        name="encode_first",
    )(*arrays)


def rest_kernel(wg, ag, wu, au, wd, ad, router, gain, first_sums, *refs):
    n = len(REST)
    pieces, slab_out = refs[: 2 * n], refs[2 * n]
    *bufs, out_buf, tall, sums, rows, slab_buf, router_buf, gain_buf = refs[2 * n + 1 : -3]
    sem, out_sem, small_sem = refs[-3:]
    chip, _ = position()

    def target(g):
        return lax.rem(chip + g, CHIPS)

    arrays = (wg, ag, wu, au, wd, ad)
    copies = [
        [
            pltpu.make_async_copy(arrays[m].at[e], bufs[m].at[e], sem.at[m, e])
            for m in (2 * a, 2 * a + 1)
        ]
        for a in range(3)
        for e in range(4)
    ]
    small = [
        pltpu.make_async_copy(router, router_buf, small_sem.at[0]),
        pltpu.make_async_copy(gain, gain_buf, small_sem.at[1]),
        pltpu.make_async_copy(first_sums, sums.at[n], small_sem.at[2]),
    ]
    for some in copies[:AHEAD]:
        for c in some:
            c.start()
    for c in small:
        c.start()
    lane = lax.broadcasted_iota(jnp.int32, (128, 128), 1)
    left = lax.broadcasted_iota(jnp.int32, (6, 128), 1) < 64

    stores = []
    for q in range(12):
        a, e = q // 4, q % 4
        for c in copies[q]:
            c.wait()
        if q + AHEAD < 12:
            for c in copies[q + AHEAD]:
                c.start()
        for i, g in enumerate(REST):
            at = pl.ds(pl.multiple_of(target(g) * 128, 128), 128)
            where = (e, slice(None), at) if a < 2 else (e, at, slice(None))
            fresh = bufs[2 * a][where] + bufs[2 * a + 1][where].astype(F32)
            total, y = normalised(fresh, 0 if a < 2 else 1)
            if a < 2:
                sums[i, q : q + 1, :] = total
                y = y.T
            elif e == 0:
                tall[i] = jnp.where(lane == 0, total, 0.0)
            else:
                tall[i] = jnp.where(lane == e, total, tall[i])
            out_buf[2 * i, q * 64 : q * 64 + 64, :] = y[:64]
            out_buf[2 * i + 1, q * 64 : q * 64 + 64, :] = y[64:]
        if q % 2 == 1:
            for i in range(n):
                send_off(out_buf, pieces, out_sem, i, q // 2, 6, stores)
    for c in small:
        c.wait()
    rows[12:16, :] = router_buf[...] * gain_buf[...]
    for i, g in enumerate((*REST, FIRST)):
        if i < n:
            sums[i, 8:16, :] = tall[i].T[0:8]
        top, bottom = sums[i, 0:6, :], sums[i, 6:12, :]
        both = (
            jnp.where(left, top, pltpu.roll(bottom, 64, 1)),
            jnp.where(left, pltpu.roll(top, 64, 1), bottom),
        )
        for c, s in enumerate(both):
            high = s.astype(BF16).astype(F32)
            rows[0:6, :] = high
            rows[6:12, :] = s - high
            slab_buf[target(g) * 2 + c] = rows[...].astype(BF16)
    copy = pltpu.make_async_copy(slab_buf, slab_out, small_sem.at[3])
    copy.start()
    for c in (*stores, copy):
        c.wait()


def encode_rest(arrays, router, gain, first_sums):
    n = len(REST)
    anywhere = pl.BlockSpec(memory_space=pl.ANY)
    return pl.pallas_call(
        rest_kernel,
        in_specs=[anywhere] * 9,
        out_specs=[anywhere] * (2 * n + 1),
        out_shape=[jax.ShapeDtypeStruct((768, 128), BF16)] * (2 * n)
        + [jax.ShapeDtypeStruct((16, 16, 128), BF16)],
        scratch_shapes=[
            pltpu.VMEM(shape, t)
            for shape in ((4, 128, 1024), (4, 128, 1024), (4, 1024, 128))
            for t in (F32, BF16)
        ]
        + [
            pltpu.VMEM((2 * n, 768, 128), BF16),
            pltpu.VMEM((n, 128, 128), F32),
            pltpu.VMEM((n + 1, 16, 128), F32),
            pltpu.VMEM((16, 128), F32),
            pltpu.VMEM((16, 16, 128), BF16),
            pltpu.VMEM((4, 128), F32),
            pltpu.VMEM((1, 128), F32),
            pltpu.SemaphoreType.DMA((6, 4)),
            pltpu.SemaphoreType.DMA((2 * n, 6)),
            pltpu.SemaphoreType.DMA((4,)),
        ],
        cost_estimate=pl.CostEstimate(
            flops=2_500_000 * n, bytes_accessed=1_600_000 * n, transcendentals=0
        ),
        name="encode_rest",
    )(*arrays, router, gain, first_sums)


def norms_kernel(slab, gate_ref, up_ref, down_ref, table_ref, factors):
    chip, core = position()
    local, total = [], jnp.zeros((6, 128), F32)
    for dz, dc in ((0, 0), *PARTNERS):
        source = lax.rem(chip + CHIPS - dz, CHIPS) * 2 + lax.bitwise_xor(core, dc)
        both = slab[source].astype(F32)
        s = both[0:6] + both[6:12]
        local.append(s)
        total = total + s
    scale = jnp.sqrt(total)
    other = pltpu.roll(scale, 64, 1)
    gate_ref[...] = scale[0:4, :64]
    up_ref[0:2, :] = scale[4:6, :64]
    up_ref[2:4, :] = other[0:2, :64]
    down_ref[...] = other[2:6, :64]
    for k in range(16):
        factors[k * 8 : k * 8 + 6, :] = jnp.sqrt(local[k] / total) * (1.0 / LIFT)
        factors[k * 8 + 6 : k * 8 + 8, :] = jnp.zeros((2, 128), F32)
    table_ref[...] = factors[...].T


def norms(slab):
    vmem = pl.BlockSpec(memory_space=pltpu.VMEM)
    return pl.pallas_call(
        norms_kernel,
        in_specs=[vmem],
        out_specs=[vmem] * 4,
        out_shape=[jax.ShapeDtypeStruct((4, 64), F32)] * 3
        + [jax.ShapeDtypeStruct((128, 128), F32)],
        scratch_shapes=[pltpu.VMEM((128, 128), F32)],
        compiler_params=pltpu.CompilerParams(vmem_limit_bytes=2 << 20),
        cost_estimate=pl.CostEstimate(
            flops=1_000_000, bytes_accessed=200_000, transcendentals=0
        ),
        name="norms",
    )(slab)


def decode_kernel(which, has_outs, table, *refs):
    n = len(which)
    pieces, refs = refs[:n], refs[n:]
    if has_outs:
        refs = refs[3:]
    outs, (out_buf, sem) = refs[:3], refs[3:]
    chip, core = position()
    partners = ((0, 0), *PARTNERS)
    stores = []
    for i, k in enumerate(which):
        dz, dc = partners[k]
        source = lax.rem(chip + CHIPS - dz, CHIPS) * 2 + lax.bitwise_xor(core, dc)
        for q in range(12):
            half, lane = q // 6, k * 8 + q % 6
            factor = table[half * 64 : half * 64 + 64, lane : lane + 1]
            y = pieces[i][q * 64 : q * 64 + 64, :].astype(F32)
            x = jnp.exp2(jnp.log2(jnp.abs(y)) * (1.0 / POWER)) * factor
            out_buf[i, q] = jnp.where(y < 0, -x, x).astype(BF16)
            if q % 4 == 3:
                a = q // 4
                at = pl.ds(pl.multiple_of(source * 128, 128), 128)
                copy = pltpu.make_async_copy(
                    out_buf.at[i, 4 * a : 4 * a + 4],
                    outs[a].at[:, :, at],
                    sem.at[i, a],
                )
                copy.start()
                stores.append(copy)
    for copy in stores:
        copy.wait()


def decode(table, pieces, which, outs):
    n = len(which)
    anywhere = pl.BlockSpec(memory_space=pl.ANY)
    vmem = pl.BlockSpec(memory_space=pltpu.VMEM)

    def kernel(*refs):
        decode_kernel(which, bool(outs), *refs)

    return pl.pallas_call(
        kernel,
        in_specs=[vmem] * (1 + n) + [anywhere] * len(outs),
        out_specs=[anywhere] * 3,
        out_shape=[jax.ShapeDtypeStruct((4, 64, 2048), BF16)] * 3,
        input_output_aliases={1 + n + a: a for a in range(len(outs))},
        scratch_shapes=[
            pltpu.VMEM((n, 12, 64, 128), BF16),
            pltpu.SemaphoreType.DMA((n, 3)),
        ],
        compiler_params=pltpu.CompilerParams(vmem_limit_bytes=8 << 20),
        cost_estimate=pl.CostEstimate(
            flops=1_200_000 * n, bytes_accessed=400_000 * n, transcendentals=200_000 * n
        ),
    )(table, *pieces, *outs)


def on_device(w_gate, avg_gate, w_up, avg_up, w_down, avg_down, router_weight, router_gain):
    arrays = (w_gate, avg_gate, w_up, avg_up, w_down, avg_down)
    router, gain = router_weight.T, router_gain[None, :]
    *some, first_sums = encode_first(arrays)
    *more, slab = encode_rest(arrays, router, gain, first_sums)
    pieces = dict(zip([(g, f) for g in (FIRST, *REST) for f in range(2)], some + more))
    slab = lax.all_to_all(slab, "fsdp", 0, 0, tiled=True)
    arrived = [pieces[0, 0]]
    for dz, dc in PARTNERS:
        pairs = [
            (2 * z + c, 2 * ((z + dz) % CHIPS) + (c ^ dc))
            for z in range(CHIPS)
            for c in range(2)
        ]
        arrived.append(lax.ppermute(pieces[dz, dc], "fsdp", pairs))
    gate_scale, up_scale, down_scale, table = norms(slab)
    router = slab[:, 12:16, :].transpose(1, 0, 2).reshape(4, 2048)
    router = jnp.broadcast_to(router[None], (16, 4, 2048))
    router = lax.all_to_all(router, "ep", 0, 0, tiled=True)
    serve_router = router.reshape(64, 2048)
    outs, done = (), 0
    for stage, end in enumerate(STAGES):
        which = tuple(range(done, end))
        outs = decode(table, [arrived[k] for k in which], which, tuple(outs))
        if stage == 0:
            table, serve_router = lax.optimization_barrier((table, serve_router))
        done = end
    gate, up, down = outs
    return (
        gate.transpose(0, 2, 1),
        up.transpose(0, 2, 1),
        down,
        gate_scale,
        up_scale,
        down_scale,
        serve_router.T,
    )


def solution(mesh):
    wide, tall = P("ep", "fsdp", None), P("ep", None, "fsdp")

    return jax.shard_map(
        on_device,
        mesh=mesh,
        in_specs=(wide, wide, wide, wide, tall, tall, P("fsdp", "ep"), P("fsdp")),
        out_specs=(tall, tall, wide, P("ep", "fsdp"), P("ep", "fsdp"), P("ep", "fsdp"), P()),
        check_vma=False,
    )
```

profile of v0, /device:TPU:1, one launch (start us, length us, event | category | flops | bytes accessed | tf_op | source)
XLA Modules:
  0.0 84.7 jit_solution(3589833732301779868)
XLA Ops:
  0.6 2.3 %encode_first.1 = (bf16[768,128]{1,0:T(8,128)(2,1)}, bf16[768,128]{1,0:T(8,128)(2,1)}, f32[16,128]{1,0:T(8,128)}) custom-call(f32[4,128,1024]{2,1,0:T(8,128)} %wg.3, bf16[4,128,1024]{2,1,0:T(8,128)(2,1)} %ag.3, f32[4,128,1024]{2,1,0:T(8,128)} %wu.3, bf16[4,128,1024]{2,1,0:T(8,128)(2,1)} %au.3, f32[4,1024,128]{2,1,0:T(8,128)} %wd.3, bf16[4,1024,128]{2,1,0:T(8,128)(2,1)} %ad.3), custom_call_target="tpu_custom_call" | custom-call | flops 2500000 | bytes 1600000 | tf_op jit(solution)/shard_map/encode_first/pallas_call | solution.py:95
  2.9 7.8 %collective-permute-start.4 = (bf16[768,128]{1,0:T(8,128)(2,1)}, bf16[768,128]{1,0:T(8,128)(2,1)S(1)}, u32[]{:S(2)}, u32[]{:S(2)}) collective-permute-start(bf16[768,128]{1,0:T(8,128)(2,1)} %get-tuple-element.49), channel_id=1, source_target_pairs={{0,8},{1,9},{2,10},{3,11},{4,12},{5,13},{6,14},{7,15},{8,0},{9,1},... | collective-permute-start | bytes 589832 | tf_op jit(solution)/shard_map/ppermute | solution.py:337
  10.7 1.0 %collective-permute-start.5 = (bf16[768,128]{1,0:T(8,128)(2,1)}, bf16[768,128]{1,0:T(8,128)(2,1)S(1)}, u32[]{:S(2)}, u32[]{:S(2)}) collective-permute-start(bf16[768,128]{1,0:T(8,128)(2,1)} %get-tuple-element.50), channel_id=1, source_target_pairs={{0,9},{1,8},{2,11},{3,10},{4,13},{5,12},{6,15},{7,14},{8,1},{9,0},... | collective-permute-start | bytes 589832 | tf_op jit(solution)/shard_map/ppermute | solution.py:337
  11.7 6.6 %encode_rest.1 = (bf16[768,128]{1,0:T(8,128)(2,1)}, bf16[768,128]{1,0:T(8,128)(2,1)}, bf16[768,128]{1,0:T(8,128)(2,1)}, bf16[768,128]{1,0:T(8,128)(2,1)}, bf16[7...) custom-call(f32[4,128,1024]{2,1,0:T(8,128)} %wg.3, ...), custom_call_target="tpu_custom_call" | custom-call | flops 17500000 | bytes 11200000 | tf_op jit(solution)/shard_map/encode_rest/pallas_call | solution.py:198
  18.4 2.7 %collective-permute-start.6 = (bf16[768,128]{1,0:T(8,128)(2,1)}, bf16[768,128]{1,0:T(8,128)(2,1)S(1)}, u32[]{:S(2)}, u32[]{:S(2)}) collective-permute-start(bf16[768,128]{1,0:T(8,128)(2,1)} %get-tuple-element.51), channel_id=1, source_target_pairs={{0,6},{1,7},{2,8},{3,9},{4,10},{5,11},{6,12},{7,13},{8,14},{9,15},... | collective-permute-start | bytes 589832 | tf_op jit(solution)/shard_map/ppermute | solution.py:337
  21.1 2.2 %collective-permute-start.7 = (bf16[768,128]{1,0:T(8,128)(2,1)}, bf16[768,128]{1,0:T(8,128)(2,1)S(1)}, u32[]{:S(2)}, u32[]{:S(2)}) collective-permute-start(bf16[768,128]{1,0:T(8,128)(2,1)} %get-tuple-element.52), channel_id=1, source_target_pairs={{0,10},{1,11},{2,12},{3,13},{4,14},{5,15},{6,0},{7,1},{8,2},{9,3},... | collective-permute-start | bytes 589832 | tf_op jit(solution)/shard_map/ppermute | solution.py:337
  23.3 0.7 collective-permute-start.8
  24.1 6.8 %all-to-all-start = ((bf16[16,16,128]{2,1,0:T(8,128)(2,1)}), bf16[16,16,128]{2,1,0:T(8,128)(2,1)S(1)}, u32[]{:S(2)}, u32[]{:S(2)}) async-start(bf16[16,16,128]{2,1,0:T(8,128)(2,1)} %get-tuple-element.41), calls=%async_computation | async-start | bytes 131072 | tf_op jit(solution)/shard_map/all_to_all | solution.py:329
  30.9 0.0 collective-permute-done.4.refs_2_
  30.9 2.6 %collective-permute-start.9 = (bf16[768,128]{1,0:T(8,128)(2,1)}, bf16[768,128]{1,0:T(8,128)(2,1)S(1)}, u32[]{:S(2)}, u32[]{:S(2)}) collective-permute-start(bf16[768,128]{1,0:T(8,128)(2,1)} %get-tuple-element.54), channel_id=1, source_target_pairs={{0,14},{1,15},{2,0},{3,1},{4,2},{5,3},{6,4},{7,5},{8,6},{9,7},{10,... | collective-permute-start | bytes 589832 | tf_op jit(solution)/shard_map/ppermute | solution.py:337
  33.5 0.0 collective-permute-done.5.refs_3_
  33.5 0.0 collective-permute-start.10
  33.5 7.9 %collective-permute-done.6.refs_4_ = bf16[768,128]{1,0:T(8,128)(2,1)S(1)} collective-permute-done((bf16[768,128]{1,0:T(8,128)(2,1)}, bf16[768,128]{1,0:T(8,128)(2,1)S(1)}, u32[]{:S(2)}, u32[]{:S(2)}) %collective-permute-start.6) | collective-permute-done | bytes 196640 | tf_op jit(solution)/shard_map/ppermute | solution.py:337
  41.4 0.0 collective-permute-start.11
  41.4 1.4 %collective-permute-done.7.refs_5_ = bf16[768,128]{1,0:T(8,128)(2,1)S(1)} collective-permute-done((bf16[768,128]{1,0:T(8,128)(2,1)}, bf16[768,128]{1,0:T(8,128)(2,1)S(1)}, u32[]{:S(2)}, u32[]{:S(2)}) %collective-permute-start.7) | collective-permute-done | bytes 196640 | tf_op jit(solution)/shard_map/ppermute | solution.py:337
  42.8 1.7 %collective-permute-start.12 = (bf16[768,128]{1,0:T(8,128)(2,1)}, bf16[768,128]{1,0:T(8,128)(2,1)S(1)}, u32[]{:S(2)}, u32[]{:S(2)}) collective-permute-start(bf16[768,128]{1,0:T(8,128)(2,1)} %get-tuple-element.57), channel_id=1, source_target_pairs={{0,4},{1,5},{2,6},{3,7},{4,8},{5,9},{6,10},{7,11},{8,12},{9,13},{1... | collective-permute-start | bytes 589832 | tf_op jit(solution)/shard_map/ppermute | solution.py:337
  44.5 1.1 %collective-permute-done.8.refs_6_ = bf16[768,128]{1,0:T(8,128)(2,1)S(1)} collective-permute-done((bf16[768,128]{1,0:T(8,128)(2,1)}, bf16[768,128]{1,0:T(8,128)(2,1)S(1)}, u32[]{:S(2)}, u32[]{:S(2)}) %collective-permute-start.8) | collective-permute-done | bytes 196640 | tf_op jit(solution)/shard_map/ppermute | solution.py:337
  45.6 2.1 %collective-permute-start.13 = (bf16[768,128]{1,0:T(8,128)(2,1)}, bf16[768,128]{1,0:T(8,128)(2,1)S(1)}, u32[]{:S(2)}, u32[]{:S(2)}) collective-permute-start(bf16[768,128]{1,0:T(8,128)(2,1)} %get-tuple-element.58), channel_id=1, source_target_pairs={{0,12},{1,13},{2,14},{3,15},{4,0},{5,1},{6,2},{7,3},{8,4},{9,5},{1... | collective-permute-start | bytes 589832 | tf_op jit(solution)/shard_map/ppermute | solution.py:337
  47.7 2.4 %all-to-all-done.slab = bf16[16,16,128]{2,1,0:T(8,128)(2,1)S(1)} async-done(((bf16[16,16,128]{2,1,0:T(8,128)(2,1)}), bf16[16,16,128]{2,1,0:T(8,128)(2,1)S(1)}, u32[]{:S(2)}, u32[]{:S(2)}) %all-to-all-start) | async-done | bytes 65568 | tf_op jit(solution)/shard_map/all_to_all | solution.py:329
  50.1 0.8 broadcast_in_dim.12
  50.9 6.8 %all-to-all-start.1 = ((bf16[16,4,2048]{2,1,0:T(4,128)(2,1)}), bf16[16,4,2048]{2,1,0:T(4,128)(2,1)S(1)}, u32[]{:S(2)}, u32[]{:S(2)}) async-start(bf16[16,4,2048]{2,1,0:T(4,128)(2,1)} %broadcast_in_dim.12), calls=%async_computation.1 | async-start | bytes 524288 | tf_op jit(solution)/shard_map/all_to_all | solution.py:341
  57.6 0.0 collective-permute-done.9.refs_7_
  57.6 0.8 collective-permute-start.14
  58.4 0.0 collective-permute-done.10.refs_8_
  58.4 0.0 collective-permute-start.2
  58.4 0.0 collective-permute-done.11.refs_9_
  58.4 3.9 %collective-permute-start.3 = (bf16[768,128]{1,0:T(8,128)(2,1)}, bf16[768,128]{1,0:T(8,128)(2,1)S(1)}, u32[]{:S(2)}, u32[]{:S(2)}) collective-permute-start(bf16[768,128]{1,0:T(8,128)(2,1)} %get-tuple-element.47), channel_id=1, source_target_pairs={{0,13},{1,12},{2,15},{3,14},{4,1},{5,0},{6,3},{7,2},{8,5},{9,4},{1... | collective-permute-start | bytes 589832 | tf_op jit(solution)/shard_map/ppermute | solution.py:337
  62.3 0.0 collective-permute-done.12.refs_10_
  62.3 0.3 collective-permute-start
  62.6 0.0 collective-permute-done.13.refs_11_
  62.6 4.5 %collective-permute-start.1 = (bf16[768,128]{1,0:T(8,128)(2,1)}, bf16[768,128]{1,0:T(8,128)(2,1)S(1)}, u32[]{:S(2)}, u32[]{:S(2)}) collective-permute-start(bf16[768,128]{1,0:T(8,128)(2,1)} %get-tuple-element.45), channel_id=1, source_target_pairs={{0,11},{1,10},{2,13},{3,12},{4,15},{5,14},{6,1},{7,0},{8,3},{9,2},... | collective-permute-start | bytes 589832 | tf_op jit(solution)/shard_map/ppermute | solution.py:337
  67.0 0.7 norms.1
  67.7 0.0 collective-permute-done.14.refs_12_
  67.7 0.0 copy-start
  67.7 0.9 %copy-done = bf16[768,128]{1,0:T(8,128)(2,1)S(1)} copy-done((bf16[768,128]{1,0:T(8,128)(2,1)S(1)}, bf16[768,128]{1,0:T(8,128)(2,1)}, u32[]{:S(2)}) %copy-start) | copy-done | bytes 196632
  68.7 2.6 %shard_map.135 = (bf16[4,64,2048]{2,1,0:T(8,128)(2,1)}, bf16[4,64,2048]{2,1,0:T(8,128)(2,1)}, bf16[4,64,2048]{2,1,0:T(8,128)(2,1)}) custom-call(f32[128,128]{1,0:T(8,128)S(1)} %get-tuple-element.43.refs_0_, bf16[768,128]{1,0:T(8,128)(2,1)S(1)} %copy-done, bf16[768,128]{1,0:T(8,128)(2,1)S(1)} %collective-permute-done.4.refs_2_, ...), custom_call_target="tpu_custom_call" | custom-call | flops 14400000 | bytes 4800000 | tf_op jit(solution)/shard_map/pallas_call | solution.py:306
  71.3 0.0 all-to-all-done.1
  71.3 0.8 reshape.18
  72.1 3.3 %collective-permute-done.2.refs_1_ = bf16[768,128]{1,0:T(8,128)(2,1)S(1)} collective-permute-done((bf16[768,128]{1,0:T(8,128)(2,1)}, bf16[768,128]{1,0:T(8,128)(2,1)S(1)}, u32[]{:S(2)}, u32[]{:S(2)}) %collective-permute-start.2) | collective-permute-done | bytes 196640 | tf_op jit(solution)/shard_map/ppermute | solution.py:337
  75.4 0.0 collective-permute-done.3.refs_2_
  75.4 1.0 %shard_map.136 = (bf16[4,64,2048]{2,1,0:T(8,128)(2,1)}, bf16[4,64,2048]{2,1,0:T(8,128)(2,1)}, bf16[4,64,2048]{2,1,0:T(8,128)(2,1)}) custom-call(f32[128,128]{1,0:T(8,128)S(1)} %get-tuple-element.43.refs_0_, bf16[768,128]{1,0:T(8,128)(2,1)S(1)} %collective-permute-done.2.refs_1_, ...), custom_call_target="tpu_custom_call", output_to_operand_aliasing={{0}: (3, {}), {1}: (4, {}), {2}: (5, {})} | custom-call | flops 2400000 | bytes 800000 | tf_op jit(solution)/shard_map/pallas_call | solution.py:306
  76.4 2.3 %collective-permute-done.refs_1_ = bf16[768,128]{1,0:T(8,128)(2,1)S(1)} collective-permute-done((bf16[768,128]{1,0:T(8,128)(2,1)}, bf16[768,128]{1,0:T(8,128)(2,1)S(1)}, u32[]{:S(2)}, u32[]{:S(2)}) %collective-permute-start) | collective-permute-done | bytes 196640 | tf_op jit(solution)/shard_map/ppermute | solution.py:337
  78.7 4.8 %collective-permute-done.1.refs_2_ = bf16[768,128]{1,0:T(8,128)(2,1)S(1)} collective-permute-done((bf16[768,128]{1,0:T(8,128)(2,1)}, bf16[768,128]{1,0:T(8,128)(2,1)S(1)}, u32[]{:S(2)}, u32[]{:S(2)}) %collective-permute-start.1) | collective-permute-done | bytes 196640 | tf_op jit(solution)/shard_map/ppermute | solution.py:337
  83.5 1.0 %shard_map.137 = (bf16[4,64,2048]{2,1,0:T(8,128)(2,1)}, bf16[4,64,2048]{2,1,0:T(8,128)(2,1)}, bf16[4,64,2048]{2,1,0:T(8,128)(2,1)}) custom-call(f32[128,128]{1,0:T(8,128)S(1)} %get-tuple-element.43.refs_0_, bf16[768,128]{1,0:T(8,128)(2,1)S(1)} %collective-permute-done.refs_1_, ...), custom_call_target="tpu_custom_call", output_to_operand_aliasing={{0}: (3, {}), {1}: (4, {}), {2}: (5, {})} | custom-call | flops 2400000 | bytes 800000 | tf_op jit(solution)/shard_map/pallas_call | solution.py:306
  (1 shorter events, 0.0 us)
Async XLA Ops:
  2.9 27.9 %collective-permute-start.4 = (bf16[768,128]{1,0:T(8,128)(2,1)}, bf16[768,128]{1,0:T(8,128)(2,1)S(1)}, u32[]{:S(2)}, u32[]{:S(2)}) collective-permute-start(bf16[768,128]{1,0:T(8,128)(2,1)} %get-tuple-element.49), channel_id=1, source_target_pairs={{0,8},{1,9},{2,10},{3,11},{4,12},{5,13},{6,14},{7,15},{8,0},{9,1},... | collective-permute-start | bytes 589832 | tf_op jit(solution)/shard_map/ppermute | solution.py:337
  10.7 22.8 %collective-permute-start.5 = (bf16[768,128]{1,0:T(8,128)(2,1)}, bf16[768,128]{1,0:T(8,128)(2,1)S(1)}, u32[]{:S(2)}, u32[]{:S(2)}) collective-permute-start(bf16[768,128]{1,0:T(8,128)(2,1)} %get-tuple-element.50), channel_id=1, source_target_pairs={{0,9},{1,8},{2,11},{3,10},{4,13},{5,12},{6,15},{7,14},{8,1},{9,0},... | collective-permute-start | bytes 589832 | tf_op jit(solution)/shard_map/ppermute | solution.py:337
  18.4 23.0 %collective-permute-start.6 = (bf16[768,128]{1,0:T(8,128)(2,1)}, bf16[768,128]{1,0:T(8,128)(2,1)S(1)}, u32[]{:S(2)}, u32[]{:S(2)}) collective-permute-start(bf16[768,128]{1,0:T(8,128)(2,1)} %get-tuple-element.51), channel_id=1, source_target_pairs={{0,6},{1,7},{2,8},{3,9},{4,10},{5,11},{6,12},{7,13},{8,14},{9,15},... | collective-permute-start | bytes 589832 | tf_op jit(solution)/shard_map/ppermute | solution.py:337
  21.1 21.6 %collective-permute-start.7 = (bf16[768,128]{1,0:T(8,128)(2,1)}, bf16[768,128]{1,0:T(8,128)(2,1)S(1)}, u32[]{:S(2)}, u32[]{:S(2)}) collective-permute-start(bf16[768,128]{1,0:T(8,128)(2,1)} %get-tuple-element.52), channel_id=1, source_target_pairs={{0,10},{1,11},{2,12},{3,13},{4,14},{5,15},{6,0},{7,1},{8,2},{9,3},... | collective-permute-start | bytes 589832 | tf_op jit(solution)/shard_map/ppermute | solution.py:337
  23.3 22.2 %collective-permute-start.8 = (bf16[768,128]{1,0:T(8,128)(2,1)}, bf16[768,128]{1,0:T(8,128)(2,1)S(1)}, u32[]{:S(2)}, u32[]{:S(2)}) collective-permute-start(bf16[768,128]{1,0:T(8,128)(2,1)} %get-tuple-element.53), channel_id=1, source_target_pairs={{0,2},{1,3},{2,4},{3,5},{4,6},{5,7},{6,8},{7,9},{8,10},{9,11},{10,... | collective-permute-start | bytes 589832 | tf_op jit(solution)/shard_map/ppermute | solution.py:337
  24.1 26.0 %all-to-all-start = ((bf16[16,16,128]{2,1,0:T(8,128)(2,1)}), bf16[16,16,128]{2,1,0:T(8,128)(2,1)S(1)}, u32[]{:S(2)}, u32[]{:S(2)}) async-start(bf16[16,16,128]{2,1,0:T(8,128)(2,1)} %get-tuple-element.41), calls=%async_computation | async-start | bytes 131072 | tf_op jit(solution)/shard_map/all_to_all | solution.py:329
  30.9 26.8 %collective-permute-start.9 = (bf16[768,128]{1,0:T(8,128)(2,1)}, bf16[768,128]{1,0:T(8,128)(2,1)S(1)}, u32[]{:S(2)}, u32[]{:S(2)}) collective-permute-start(bf16[768,128]{1,0:T(8,128)(2,1)} %get-tuple-element.54), channel_id=1, source_target_pairs={{0,14},{1,15},{2,0},{3,1},{4,2},{5,3},{6,4},{7,5},{8,6},{9,7},{10,... | collective-permute-start | bytes 589832 | tf_op jit(solution)/shard_map/ppermute | solution.py:337
  33.5 24.9 %collective-permute-start.10 = (bf16[768,128]{1,0:T(8,128)(2,1)}, bf16[768,128]{1,0:T(8,128)(2,1)S(1)}, u32[]{:S(2)}, u32[]{:S(2)}) collective-permute-start(bf16[768,128]{1,0:T(8,128)(2,1)} %get-tuple-element.55), channel_id=1, source_target_pairs={{0,3},{1,2},{2,5},{3,4},{4,7},{5,6},{6,9},{7,8},{8,11},{9,10},{10,... | collective-permute-start | bytes 589832 | tf_op jit(solution)/shard_map/ppermute | solution.py:337
  41.4 17.0 %collective-permute-start.11 = (bf16[768,128]{1,0:T(8,128)(2,1)}, bf16[768,128]{1,0:T(8,128)(2,1)S(1)}, u32[]{:S(2)}, u32[]{:S(2)}) collective-permute-start(bf16[768,128]{1,0:T(8,128)(2,1)} %get-tuple-element.56), channel_id=1, source_target_pairs={{0,15},{1,14},{2,1},{3,0},{4,3},{5,2},{6,5},{7,4},{8,7},{9,6},{10,... | collective-permute-start | bytes 589832 | tf_op jit(solution)/shard_map/ppermute | solution.py:337
  42.8 19.5 %collective-permute-start.12 = (bf16[768,128]{1,0:T(8,128)(2,1)}, bf16[768,128]{1,0:T(8,128)(2,1)S(1)}, u32[]{:S(2)}, u32[]{:S(2)}) collective-permute-start(bf16[768,128]{1,0:T(8,128)(2,1)} %get-tuple-element.57), channel_id=1, source_target_pairs={{0,4},{1,5},{2,6},{3,7},{4,8},{5,9},{6,10},{7,11},{8,12},{9,13},{1... | collective-permute-start | bytes 589832 | tf_op jit(solution)/shard_map/ppermute | solution.py:337
  45.6 17.0 %collective-permute-start.13 = (bf16[768,128]{1,0:T(8,128)(2,1)}, bf16[768,128]{1,0:T(8,128)(2,1)S(1)}, u32[]{:S(2)}, u32[]{:S(2)}) collective-permute-start(bf16[768,128]{1,0:T(8,128)(2,1)} %get-tuple-element.58), channel_id=1, source_target_pairs={{0,12},{1,13},{2,14},{3,15},{4,0},{5,1},{6,2},{7,3},{8,4},{9,5},{1... | collective-permute-start | bytes 589832 | tf_op jit(solution)/shard_map/ppermute | solution.py:337
  50.9 20.4 %all-to-all-start.1 = ((bf16[16,4,2048]{2,1,0:T(4,128)(2,1)}), bf16[16,4,2048]{2,1,0:T(4,128)(2,1)S(1)}, u32[]{:S(2)}, u32[]{:S(2)}) async-start(bf16[16,4,2048]{2,1,0:T(4,128)(2,1)} %broadcast_in_dim.12), calls=%async_computation.1 | async-start | bytes 524288 | tf_op jit(solution)/shard_map/all_to_all | solution.py:341
  57.6 10.1 %collective-permute-start.14 = (bf16[768,128]{1,0:T(8,128)(2,1)}, bf16[768,128]{1,0:T(8,128)(2,1)S(1)}, u32[]{:S(2)}, u32[]{:S(2)}) collective-permute-start(bf16[768,128]{1,0:T(8,128)(2,1)} %get-tuple-element.59), channel_id=1, source_target_pairs={{0,1},{1,0},{2,3},{3,2},{4,5},{5,4},{6,7},{7,6},{8,9},{9,8},{10,11... | collective-permute-start | bytes 589832 | tf_op jit(solution)/shard_map/ppermute | solution.py:337
  58.4 17.0 %collective-permute-start.2 = (bf16[768,128]{1,0:T(8,128)(2,1)}, bf16[768,128]{1,0:T(8,128)(2,1)S(1)}, u32[]{:S(2)}, u32[]{:S(2)}) collective-permute-start(bf16[768,128]{1,0:T(8,128)(2,1)} %get-tuple-element.46), channel_id=1, source_target_pairs={{0,5},{1,4},{2,7},{3,6},{4,9},{5,8},{6,11},{7,10},{8,13},{9,12},{1... | collective-permute-start | bytes 589832 | tf_op jit(solution)/shard_map/ppermute | solution.py:337
  58.4 17.0 %collective-permute-start.3 = (bf16[768,128]{1,0:T(8,128)(2,1)}, bf16[768,128]{1,0:T(8,128)(2,1)S(1)}, u32[]{:S(2)}, u32[]{:S(2)}) collective-permute-start(bf16[768,128]{1,0:T(8,128)(2,1)} %get-tuple-element.47), channel_id=1, source_target_pairs={{0,13},{1,12},{2,15},{3,14},{4,1},{5,0},{6,3},{7,2},{8,5},{9,4},{1... | collective-permute-start | bytes 589832 | tf_op jit(solution)/shard_map/ppermute | solution.py:337
  62.3 16.5 %collective-permute-start = (bf16[768,128]{1,0:T(8,128)(2,1)}, bf16[768,128]{1,0:T(8,128)(2,1)S(1)}, u32[]{:S(2)}, u32[]{:S(2)}) collective-permute-start(bf16[768,128]{1,0:T(8,128)(2,1)} %get-tuple-element.44), channel_id=1, source_target_pairs={{0,7},{1,6},{2,9},{3,8},{4,11},{5,10},{6,13},{7,12},{8,15},{9,14},... | collective-permute-start | bytes 589832 | tf_op jit(solution)/shard_map/ppermute | solution.py:337
  62.6 21.0 %collective-permute-start.1 = (bf16[768,128]{1,0:T(8,128)(2,1)}, bf16[768,128]{1,0:T(8,128)(2,1)S(1)}, u32[]{:S(2)}, u32[]{:S(2)}) collective-permute-start(bf16[768,128]{1,0:T(8,128)(2,1)} %get-tuple-element.45), channel_id=1, source_target_pairs={{0,11},{1,10},{2,13},{3,12},{4,15},{5,14},{6,1},{7,0},{8,3},{9,2},... | collective-permute-start | bytes 589832 | tf_op jit(solution)/shard_map/ppermute | solution.py:337
  67.7 0.9 %copy-start = (bf16[768,128]{1,0:T(8,128)(2,1)S(1)}, bf16[768,128]{1,0:T(8,128)(2,1)}, u32[]{:S(2)}) copy-start(bf16[768,128]{1,0:T(8,128)(2,1)} %get-tuple-element.48.refs_1_) | copy-start | bytes 589828
where the time goes:
time: 86.2 us; the launch traced here: 84.7 us
  starting transfers between devices  43.9 us (51%)
  waiting for transfers between devices  23.2 us (27%)
  Pallas kernels  14.2 us (16%)
  local copies, waits for them, and re-layouts  2.51 us (3%)
  between operations  0.88 us (1%)
    ppermute x15, starting transfers between devices, on_device(): arrived.append(lax.ppermute(pieces[dz, dc], 'fsdp', pairs))  30.3 us
    ppermute x15, waiting for transfers between devices, on_device(): arrived.append(lax.ppermute(pieces[dz, dc], 'fsdp', pairs))  20.8 us
    all_to_all x1, starting transfers between devices, on_device(): slab = lax.all_to_all(slab, 'fsdp', 0, 0, tiled=True)  6.79 us
    all_to_all x1, starting transfers between devices, on_device(): router = lax.all_to_all(router, 'ep', 0, 0, tiled=True)  6.75 us
    pallas_call x1, Pallas kernels, encode_rest(): pl.pallas_call(rest_kernel, in_specs=[anywhere] * 9, out_specs=[anywhere]...  6.64 us
    pallas_call x3, Pallas kernels, decode(): pl.pallas_call(kernel, in_specs=[vmem] * (1 + n) + [anywhere] * len(outs)...  4.63 us
    all_to_all x1, waiting for transfers between devices, on_device(): slab = lax.all_to_all(slab, 'fsdp', 0, 0, tiled=True)  2.39 us
    pallas_call x1, Pallas kernels, encode_first(): pl.pallas_call(first_kernel, in_specs=[anywhere] * 6, out_specs=[anywhere...  2.28 us
  transfers between devices with their start and end apart: 17, of which 7 were waited for; matrix products, arithmetic and copies ran while one was open for 2% of the time, Pallas kernels for 13%

commit v1 on v0

--- a/solution.py
+++ b/solution.py
@@ -13,11 +13,11 @@
 F32, BF16 = jnp.float32, jnp.bfloat16
 
 PARTNERS = (
-    (4, 0), (4, 1), (3, 0), (5, 0), (1, 0), (7, 0), (1, 1), (7, 1),
-    (2, 0), (6, 0), (0, 1), (2, 1), (6, 1), (3, 1), (5, 1),
+    (3, 0), (3, 1), (4, 0), (4, 1), (2, 0), (6, 0), (1, 0), (7, 0),
+    (2, 1), (6, 1), (1, 1), (7, 1), (0, 1), (5, 0), (5, 1),
 )
-FIRST = 4
-REST = (3, 5, 2, 6, 0, 1, 7)
+FIRST = 3
+REST = (4, 5, 2, 6, 0, 1, 7)
 STAGES = (12, 14, 16)
 AHEAD = 8
 
@@ -25,6 +25,16 @@
 def position():
     me = lax.axis_index("fsdp")
     return lax.shift_right_logical(me, 1), lax.bitwise_and(me, 1)
+
+
+def away(chip, core, g):
+    return lax.rem(chip + jnp.where(core == 0, g, CHIPS - g), CHIPS)
+
+
+def source_of(chip, core, partner):
+    dz, dc = partner
+    sender = lax.bitwise_xor(core, dc)
+    return away(chip, 1 - sender, dz) * 2 + sender
 
 
 def power(x):
@@ -56,8 +66,8 @@
 
 def first_kernel(wg, ag, wu, au, wd, ad, piece_0, piece_1, sums_out, *scratch):
     *bufs, out_buf, sums, sem, out_sem, sums_sem = scratch
-    chip, _ = position()
-    at = pl.ds(pl.multiple_of(lax.rem(chip + FIRST, CHIPS) * 128, 128), 128)
+    chip, core = position()
+    at = pl.ds(pl.multiple_of(away(chip, core, FIRST) * 128, 128), 128)
     views = [r.at[:, :, at] for r in (wg, ag, wu, au)]
     views += [r.at[:, at, :] for r in (wd, ad)]
     copies = [
@@ -118,10 +128,10 @@
     pieces, slab_out = refs[: 2 * n], refs[2 * n]
     *bufs, out_buf, tall, sums, rows, slab_buf, router_buf, gain_buf = refs[2 * n + 1 : -3]
     sem, out_sem, small_sem = refs[-3:]
-    chip, _ = position()
+    chip, core = position()
 
     def target(g):
-        return lax.rem(chip + g, CHIPS)
+        return away(chip, core, g)
 
     arrays = (wg, ag, wu, au, wd, ad)
     copies = [
@@ -228,9 +238,8 @@
 def norms_kernel(slab, gate_ref, up_ref, down_ref, table_ref, factors):
     chip, core = position()
     local, total = [], jnp.zeros((6, 128), F32)
-    for dz, dc in ((0, 0), *PARTNERS):
-        source = lax.rem(chip + CHIPS - dz, CHIPS) * 2 + lax.bitwise_xor(core, dc)
-        both = slab[source].astype(F32)
+    for partner in ((0, 0), *PARTNERS):
+        both = slab[source_of(chip, core, partner)].astype(F32)
         s = both[0:6] + both[6:12]
         local.append(s)
         total = total + s
@@ -273,8 +282,7 @@
     partners = ((0, 0), *PARTNERS)
     stores = []
     for i, k in enumerate(which):
-        dz, dc = partners[k]
-        source = lax.rem(chip + CHIPS - dz, CHIPS) * 2 + lax.bitwise_xor(core, dc)
+        source = source_of(chip, core, partners[k])
         for q in range(12):
             half, lane = q // 6, k * 8 + q % 6
             factor = table[half * 64 : half * 64 + 64, lane : lane + 1]
@@ -330,7 +338,7 @@
     arrived = [pieces[0, 0]]
     for dz, dc in PARTNERS:
         pairs = [
-            (2 * z + c, 2 * ((z + dz) % CHIPS) + (c ^ dc))
+            (2 * z + c, 2 * ((z + (dz, CHIPS - dz)[c]) % CHIPS) + (c ^ dc))
             for z in range(CHIPS)
             for c in range(2)
         ]

time: 86.2 us -> 84.7 us (0.983)
  the two profiles are of different devices: /device:TPU:1 before, /device:TPU:2 now
where the time goes in v1:
time: 84.7 us; the launch traced here: 84.4 us
  starting transfers between devices  51.2 us (60%)
  waiting for transfers between devices  15.6 us (18%)
  Pallas kernels  14.3 us (17%)
  local copies, waits for them, and re-layouts  2.51 us (3%)
  between operations  0.9 us (1%)
    ppermute x15, starting transfers between devices, on_device(): arrived.append(lax.ppermute(pieces[dz, dc], 'fsdp', pairs))  36.9 us
    ppermute x15, waiting for transfers between devices, on_device(): arrived.append(lax.ppermute(pieces[dz, dc], 'fsdp', pairs))  15.6 us
    all_to_all x1, starting transfers between devices, on_device(): router = lax.all_to_all(router, 'ep', 0, 0, tiled=True)  7.48 us
    all_to_all x1, starting transfers between devices, on_device(): slab = lax.all_to_all(slab, 'fsdp', 0, 0, tiled=True)  6.76 us
    pallas_call x1, Pallas kernels, encode_rest(): pl.pallas_call(rest_kernel, in_specs=[anywhere] * 9, out_specs=[anywhere]...  6.64 us
    pallas_call x3, Pallas kernels, decode(): pl.pallas_call(kernel, in_specs=[vmem] * (1 + n) + [anywhere] * len(outs)...  4.62 us
    pallas_call x1, Pallas kernels, encode_first(): pl.pallas_call(first_kernel, in_specs=[anywhere] * 6, out_specs=[anywhere...  2.28 us
  transfers between devices with their start and end apart: 17, of which 3 were waited for; matrix products, arithmetic and copies ran while one was open for 2% of the time, Pallas kernels for 13%

profile of v1, /device:TPU:2, one launch (start us, length us, event | category | flops | bytes accessed | tf_op | source)
XLA Modules:
  0.0 84.4 jit_solution(16704433213016974123)
XLA Ops:
  0.6 2.3 %encode_first.1 = (bf16[768,128]{1,0:T(8,128)(2,1)}, bf16[768,128]{1,0:T(8,128)(2,1)}, f32[16,128]{1,0:T(8,128)}) custom-call(f32[4,128,1024]{2,1,0:T(8,128)} %wg.3, bf16[4,128,1024]{2,1,0:T(8,128)(2,1)} %ag.3, f32[4,128,1024]{2,1,0:T(8,128)} %wu.3, bf16[4,128,1024]{2,1,0:T(8,128)(2,1)} %au.3, f32[4,1024,128]{2,1,0:T(8,128)} %wd.3, bf16[4,1024,128]{2,1,0:T(8,128)(2,1)} %ad.3), custom_call_target="tpu_custom_call" | custom-call | flops 2500000 | bytes 1600000 | tf_op jit(solution)/shard_map/encode_first/pallas_call | solution.py:105
  2.9 4.7 %collective-permute-start.4 = (bf16[768,128]{1,0:T(8,128)(2,1)}, bf16[768,128]{1,0:T(8,128)(2,1)S(1)}, u32[]{:S(2)}, u32[]{:S(2)}) collective-permute-start(bf16[768,128]{1,0:T(8,128)(2,1)} %get-tuple-element.49), channel_id=1, source_target_pairs={{0,6},{1,11},{2,8},{3,13},{4,10},{5,15},{6,12},{7,1},{8,14},{9,3},... | collective-permute-start | bytes 589832 | tf_op jit(solution)/shard_map/ppermute | solution.py:345
  7.6 0.0 collective-permute-start.5
  7.6 6.6 %encode_rest.1 = (bf16[768,128]{1,0:T(8,128)(2,1)}, bf16[768,128]{1,0:T(8,128)(2,1)}, bf16[768,128]{1,0:T(8,128)(2,1)}, bf16[768,128]{1,0:T(8,128)(2,1)}, bf16[7...) custom-call(f32[4,128,1024]{2,1,0:T(8,128)} %wg.3, ...), custom_call_target="tpu_custom_call" | custom-call | flops 17500000 | bytes 11200000 | tf_op jit(solution)/shard_map/encode_rest/pallas_call | solution.py:208
  14.3 5.6 %collective-permute-start.6 = (bf16[768,128]{1,0:T(8,128)(2,1)}, bf16[768,128]{1,0:T(8,128)(2,1)S(1)}, u32[]{:S(2)}, u32[]{:S(2)}) collective-permute-start(bf16[768,128]{1,0:T(8,128)(2,1)} %get-tuple-element.51), channel_id=1, source_target_pairs={{0,8},{1,9},{2,10},{3,11},{4,12},{5,13},{6,14},{7,15},{8,0},{9,1},... | collective-permute-start | bytes 589832 | tf_op jit(solution)/shard_map/ppermute | solution.py:345
  19.9 2.0 %collective-permute-start.7 = (bf16[768,128]{1,0:T(8,128)(2,1)}, bf16[768,128]{1,0:T(8,128)(2,1)S(1)}, u32[]{:S(2)}, u32[]{:S(2)}) collective-permute-start(bf16[768,128]{1,0:T(8,128)(2,1)} %get-tuple-element.52), channel_id=1, source_target_pairs={{0,9},{1,8},{2,11},{3,10},{4,13},{5,12},{6,15},{7,14},{8,1},{9,0},... | collective-permute-start | bytes 589832 | tf_op jit(solution)/shard_map/ppermute | solution.py:345
  22.0 1.5 %collective-permute-start.8 = (bf16[768,128]{1,0:T(8,128)(2,1)}, bf16[768,128]{1,0:T(8,128)(2,1)S(1)}, u32[]{:S(2)}, u32[]{:S(2)}) collective-permute-start(bf16[768,128]{1,0:T(8,128)(2,1)} %get-tuple-element.53), channel_id=1, source_target_pairs={{0,4},{1,13},{2,6},{3,15},{4,8},{5,1},{6,10},{7,3},{8,12},{9,5},{1... | collective-permute-start | bytes 589832 | tf_op jit(solution)/shard_map/ppermute | solution.py:345
  23.4 6.8 %all-to-all-start = ((bf16[16,16,128]{2,1,0:T(8,128)(2,1)}), bf16[16,16,128]{2,1,0:T(8,128)(2,1)S(1)}, u32[]{:S(2)}, u32[]{:S(2)}) async-start(bf16[16,16,128]{2,1,0:T(8,128)(2,1)} %get-tuple-element.41), calls=%async_computation | async-start | bytes 131072 | tf_op jit(solution)/shard_map/all_to_all | solution.py:337
  30.2 0.0 collective-permute-done.4.refs_2_
  30.2 4.1 %collective-permute-start.9 = (bf16[768,128]{1,0:T(8,128)(2,1)}, bf16[768,128]{1,0:T(8,128)(2,1)S(1)}, u32[]{:S(2)}, u32[]{:S(2)}) collective-permute-start(bf16[768,128]{1,0:T(8,128)(2,1)} %get-tuple-element.54), channel_id=1, source_target_pairs={{0,12},{1,5},{2,14},{3,7},{4,0},{5,9},{6,2},{7,11},{8,4},{9,13},{1... | collective-permute-start | bytes 589832 | tf_op jit(solution)/shard_map/ppermute | solution.py:345
  34.3 0.0 collective-permute-done.5.refs_3_
  34.3 0.6 collective-permute-start.10
  34.9 0.0 collective-permute-done.6.refs_4_
  34.9 3.0 %collective-permute-start.11 = (bf16[768,128]{1,0:T(8,128)(2,1)}, bf16[768,128]{1,0:T(8,128)(2,1)S(1)}, u32[]{:S(2)}, u32[]{:S(2)}) collective-permute-start(bf16[768,128]{1,0:T(8,128)(2,1)} %get-tuple-element.56), channel_id=1, source_target_pairs={{0,14},{1,3},{2,0},{3,5},{4,2},{5,7},{6,4},{7,9},{8,6},{9,11},{10,... | collective-permute-start | bytes 589832 | tf_op jit(solution)/shard_map/ppermute | solution.py:345
  37.9 5.3 %collective-permute-done.7.refs_5_ = bf16[768,128]{1,0:T(8,128)(2,1)S(1)} collective-permute-done((bf16[768,128]{1,0:T(8,128)(2,1)}, bf16[768,128]{1,0:T(8,128)(2,1)S(1)}, u32[]{:S(2)}, u32[]{:S(2)}) %collective-permute-start.7) | collective-permute-done | bytes 196640 | tf_op jit(solution)/shard_map/ppermute | solution.py:345
  43.2 0.0 collective-permute-start.12
  43.2 2.1 %collective-permute-done.8.refs_6_ = bf16[768,128]{1,0:T(8,128)(2,1)S(1)} collective-permute-done((bf16[768,128]{1,0:T(8,128)(2,1)}, bf16[768,128]{1,0:T(8,128)(2,1)S(1)}, u32[]{:S(2)}, u32[]{:S(2)}) %collective-permute-start.8) | collective-permute-done | bytes 196640 | tf_op jit(solution)/shard_map/ppermute | solution.py:345
  45.3 7.5 %collective-permute-start.13 = (bf16[768,128]{1,0:T(8,128)(2,1)}, bf16[768,128]{1,0:T(8,128)(2,1)S(1)}, u32[]{:S(2)}, u32[]{:S(2)}) collective-permute-start(bf16[768,128]{1,0:T(8,128)(2,1)} %get-tuple-element.58), channel_id=1, source_target_pairs={{0,13},{1,4},{2,15},{3,6},{4,1},{5,8},{6,3},{7,10},{8,5},{9,12},{1... | collective-permute-start | bytes 589832 | tf_op jit(solution)/shard_map/ppermute | solution.py:345
  52.8 0.0 all-to-all-done.slab
  52.8 0.8 broadcast_in_dim.12
  53.6 7.5 %all-to-all-start.1 = ((bf16[16,4,2048]{2,1,0:T(4,128)(2,1)}), bf16[16,4,2048]{2,1,0:T(4,128)(2,1)S(1)}, u32[]{:S(2)}, u32[]{:S(2)}) async-start(bf16[16,4,2048]{2,1,0:T(4,128)(2,1)} %broadcast_in_dim.12), calls=%async_computation.1 | async-start | bytes 524288 | tf_op jit(solution)/shard_map/all_to_all | solution.py:349
  61.1 0.0 collective-permute-done.9.refs_7_
  61.1 0.3 collective-permute-start.14
  61.4 0.0 collective-permute-done.10.refs_8_
  61.4 2.8 %collective-permute-start.2 = (bf16[768,128]{1,0:T(8,128)(2,1)}, bf16[768,128]{1,0:T(8,128)(2,1)S(1)}, u32[]{:S(2)}, u32[]{:S(2)}) collective-permute-start(bf16[768,128]{1,0:T(8,128)(2,1)} %get-tuple-element.46), channel_id=1, source_target_pairs={{0,15},{1,2},{2,1},{3,4},{4,3},{5,6},{6,5},{7,8},{8,7},{9,10},{10,... | collective-permute-start | bytes 589832 | tf_op jit(solution)/shard_map/ppermute | solution.py:345
  64.2 0.0 collective-permute-done.11.refs_9_
  64.2 0.0 collective-permute-start.3
  64.2 0.0 collective-permute-done.12.refs_10_
  64.2 1.5 %collective-permute-start = (bf16[768,128]{1,0:T(8,128)(2,1)}, bf16[768,128]{1,0:T(8,128)(2,1)S(1)}, u32[]{:S(2)}, u32[]{:S(2)}) collective-permute-start(bf16[768,128]{1,0:T(8,128)(2,1)} %get-tuple-element.44), channel_id=1, source_target_pairs={{0,10},{1,7},{2,12},{3,9},{4,14},{5,11},{6,0},{7,13},{8,2},{9,15},... | collective-permute-start | bytes 589832 | tf_op jit(solution)/shard_map/ppermute | solution.py:345
  65.6 0.0 collective-permute-done.13.refs_11_
  65.7 3.4 %collective-permute-start.1 = (bf16[768,128]{1,0:T(8,128)(2,1)}, bf16[768,128]{1,0:T(8,128)(2,1)S(1)}, u32[]{:S(2)}, u32[]{:S(2)}) collective-permute-start(bf16[768,128]{1,0:T(8,128)(2,1)} %get-tuple-element.45), channel_id=1, source_target_pairs={{0,11},{1,6},{2,13},{3,8},{4,15},{5,10},{6,1},{7,12},{8,3},{9,14},... | collective-permute-start | bytes 589832 | tf_op jit(solution)/shard_map/ppermute | solution.py:345
  69.1 0.7 norms.1
  69.8 0.0 collective-permute-done.14.refs_12_
  69.8 0.0 copy-start
  69.8 0.9 %copy-done = bf16[768,128]{1,0:T(8,128)(2,1)S(1)} copy-done((bf16[768,128]{1,0:T(8,128)(2,1)S(1)}, bf16[768,128]{1,0:T(8,128)(2,1)}, u32[]{:S(2)}) %copy-start) | copy-done | bytes 196632
  70.7 2.6 %shard_map.135 = (bf16[4,64,2048]{2,1,0:T(8,128)(2,1)}, bf16[4,64,2048]{2,1,0:T(8,128)(2,1)}, bf16[4,64,2048]{2,1,0:T(8,128)(2,1)}) custom-call(f32[128,128]{1,0:T(8,128)S(1)} %get-tuple-element.43.refs_0_, bf16[768,128]{1,0:T(8,128)(2,1)S(1)} %copy-done, bf16[768,128]{1,0:T(8,128)(2,1)S(1)} %collective-permute-done.4.refs_2_, ...), custom_call_target="tpu_custom_call" | custom-call | flops 14400000 | bytes 4800000 | tf_op jit(solution)/shard_map/pallas_call | solution.py:314
  73.3 0.0 all-to-all-done.1
  73.3 0.8 reshape.18
  74.1 0.0 collective-permute-done.2.refs_1_
  74.1 0.0 collective-permute-done.3.refs_2_
  74.1 1.0 %shard_map.136 = (bf16[4,64,2048]{2,1,0:T(8,128)(2,1)}, bf16[4,64,2048]{2,1,0:T(8,128)(2,1)}, bf16[4,64,2048]{2,1,0:T(8,128)(2,1)}) custom-call(f32[128,128]{1,0:T(8,128)S(1)} %get-tuple-element.43.refs_0_, bf16[768,128]{1,0:T(8,128)(2,1)S(1)} %collective-permute-done.2.refs_1_, ...), custom_call_target="tpu_custom_call", output_to_operand_aliasing={{0}: (3, {}), {1}: (4, {}), {2}: (5, {})} | custom-call | flops 2400000 | bytes 800000 | tf_op jit(solution)/shard_map/pallas_call | solution.py:314
  75.1 0.0 collective-permute-done.refs_1_
  75.1 8.1 %collective-permute-done.1.refs_2_ = bf16[768,128]{1,0:T(8,128)(2,1)S(1)} collective-permute-done((bf16[768,128]{1,0:T(8,128)(2,1)}, bf16[768,128]{1,0:T(8,128)(2,1)S(1)}, u32[]{:S(2)}, u32[]{:S(2)}) %collective-permute-start.1) | collective-permute-done | bytes 196640 | tf_op jit(solution)/shard_map/ppermute | solution.py:345
  83.2 1.0 %shard_map.137 = (bf16[4,64,2048]{2,1,0:T(8,128)(2,1)}, bf16[4,64,2048]{2,1,0:T(8,128)(2,1)}, bf16[4,64,2048]{2,1,0:T(8,128)(2,1)}) custom-call(f32[128,128]{1,0:T(8,128)S(1)} %get-tuple-element.43.refs_0_, bf16[768,128]{1,0:T(8,128)(2,1)S(1)} %collective-permute-done.refs_1_, ...), custom_call_target="tpu_custom_call", output_to_operand_aliasing={{0}: (3, {}), {1}: (4, {}), {2}: (5, {})} | custom-call | flops 2400000 | bytes 800000 | tf_op jit(solution)/shard_map/pallas_call | solution.py:314
  (1 shorter events, 0.0 us)
Async XLA Ops:
  2.9 27.3 %collective-permute-start.4 = (bf16[768,128]{1,0:T(8,128)(2,1)}, bf16[768,128]{1,0:T(8,128)(2,1)S(1)}, u32[]{:S(2)}, u32[]{:S(2)}) collective-permute-start(bf16[768,128]{1,0:T(8,128)(2,1)} %get-tuple-element.49), channel_id=1, source_target_pairs={{0,6},{1,11},{2,8},{3,13},{4,10},{5,15},{6,12},{7,1},{8,14},{9,3},... | collective-permute-start | bytes 589832 | tf_op jit(solution)/shard_map/ppermute | solution.py:345
  7.6 26.7 %collective-permute-start.5 = (bf16[768,128]{1,0:T(8,128)(2,1)}, bf16[768,128]{1,0:T(8,128)(2,1)S(1)}, u32[]{:S(2)}, u32[]{:S(2)}) collective-permute-start(bf16[768,128]{1,0:T(8,128)(2,1)} %get-tuple-element.50), channel_id=1, source_target_pairs={{0,7},{1,10},{2,9},{3,12},{4,11},{5,14},{6,13},{7,0},{8,15},{9,2},... | collective-permute-start | bytes 589832 | tf_op jit(solution)/shard_map/ppermute | solution.py:345
  14.3 20.6 %collective-permute-start.6 = (bf16[768,128]{1,0:T(8,128)(2,1)}, bf16[768,128]{1,0:T(8,128)(2,1)S(1)}, u32[]{:S(2)}, u32[]{:S(2)}) collective-permute-start(bf16[768,128]{1,0:T(8,128)(2,1)} %get-tuple-element.51), channel_id=1, source_target_pairs={{0,8},{1,9},{2,10},{3,11},{4,12},{5,13},{6,14},{7,15},{8,0},{9,1},... | collective-permute-start | bytes 589832 | tf_op jit(solution)/shard_map/ppermute | solution.py:345
  19.9 23.3 %collective-permute-start.7 = (bf16[768,128]{1,0:T(8,128)(2,1)}, bf16[768,128]{1,0:T(8,128)(2,1)S(1)}, u32[]{:S(2)}, u32[]{:S(2)}) collective-permute-start(bf16[768,128]{1,0:T(8,128)(2,1)} %get-tuple-element.52), channel_id=1, source_target_pairs={{0,9},{1,8},{2,11},{3,10},{4,13},{5,12},{6,15},{7,14},{8,1},{9,0},... | collective-permute-start | bytes 589832 | tf_op jit(solution)/shard_map/ppermute | solution.py:345
  22.0 23.3 %collective-permute-start.8 = (bf16[768,128]{1,0:T(8,128)(2,1)}, bf16[768,128]{1,0:T(8,128)(2,1)S(1)}, u32[]{:S(2)}, u32[]{:S(2)}) collective-permute-start(bf16[768,128]{1,0:T(8,128)(2,1)} %get-tuple-element.53), channel_id=1, source_target_pairs={{0,4},{1,13},{2,6},{3,15},{4,8},{5,1},{6,10},{7,3},{8,12},{9,5},{1... | collective-permute-start | bytes 589832 | tf_op jit(solution)/shard_map/ppermute | solution.py:345
  23.4 29.4 %all-to-all-start = ((bf16[16,16,128]{2,1,0:T(8,128)(2,1)}), bf16[16,16,128]{2,1,0:T(8,128)(2,1)S(1)}, u32[]{:S(2)}, u32[]{:S(2)}) async-start(bf16[16,16,128]{2,1,0:T(8,128)(2,1)} %get-tuple-element.41), calls=%async_computation | async-start | bytes 131072 | tf_op jit(solution)/shard_map/all_to_all | solution.py:337
  30.2 30.9 %collective-permute-start.9 = (bf16[768,128]{1,0:T(8,128)(2,1)}, bf16[768,128]{1,0:T(8,128)(2,1)S(1)}, u32[]{:S(2)}, u32[]{:S(2)}) collective-permute-start(bf16[768,128]{1,0:T(8,128)(2,1)} %get-tuple-element.54), channel_id=1, source_target_pairs={{0,12},{1,5},{2,14},{3,7},{4,0},{5,9},{6,2},{7,11},{8,4},{9,13},{1... | collective-permute-start | bytes 589832 | tf_op jit(solution)/shard_map/ppermute | solution.py:345
  34.3 27.1 %collective-permute-start.10 = (bf16[768,128]{1,0:T(8,128)(2,1)}, bf16[768,128]{1,0:T(8,128)(2,1)S(1)}, u32[]{:S(2)}, u32[]{:S(2)}) collective-permute-start(bf16[768,128]{1,0:T(8,128)(2,1)} %get-tuple-element.55), channel_id=1, source_target_pairs={{0,2},{1,15},{2,4},{3,1},{4,6},{5,3},{6,8},{7,5},{8,10},{9,7},{10,... | collective-permute-start | bytes 589832 | tf_op jit(solution)/shard_map/ppermute | solution.py:345
  34.9 29.3 %collective-permute-start.11 = (bf16[768,128]{1,0:T(8,128)(2,1)}, bf16[768,128]{1,0:T(8,128)(2,1)S(1)}, u32[]{:S(2)}, u32[]{:S(2)}) collective-permute-start(bf16[768,128]{1,0:T(8,128)(2,1)} %get-tuple-element.56), channel_id=1, source_target_pairs={{0,14},{1,3},{2,0},{3,5},{4,2},{5,7},{6,4},{7,9},{8,6},{9,11},{10,... | collective-permute-start | bytes 589832 | tf_op jit(solution)/shard_map/ppermute | solution.py:345
  43.2 21.0 %collective-permute-start.12 = (bf16[768,128]{1,0:T(8,128)(2,1)}, bf16[768,128]{1,0:T(8,128)(2,1)S(1)}, u32[]{:S(2)}, u32[]{:S(2)}) collective-permute-start(bf16[768,128]{1,0:T(8,128)(2,1)} %get-tuple-element.57), channel_id=1, source_target_pairs={{0,5},{1,12},{2,7},{3,14},{4,9},{5,0},{6,11},{7,2},{8,13},{9,4},{1... | collective-permute-start | bytes 589832 | tf_op jit(solution)/shard_map/ppermute | solution.py:345
  45.3 20.3 %collective-permute-start.13 = (bf16[768,128]{1,0:T(8,128)(2,1)}, bf16[768,128]{1,0:T(8,128)(2,1)S(1)}, u32[]{:S(2)}, u32[]{:S(2)}) collective-permute-start(bf16[768,128]{1,0:T(8,128)(2,1)} %get-tuple-element.58), channel_id=1, source_target_pairs={{0,13},{1,4},{2,15},{3,6},{4,1},{5,8},{6,3},{7,10},{8,5},{9,12},{1... | collective-permute-start | bytes 589832 | tf_op jit(solution)/shard_map/ppermute | solution.py:345
  53.6 19.7 %all-to-all-start.1 = ((bf16[16,4,2048]{2,1,0:T(4,128)(2,1)}), bf16[16,4,2048]{2,1,0:T(4,128)(2,1)S(1)}, u32[]{:S(2)}, u32[]{:S(2)}) async-start(bf16[16,4,2048]{2,1,0:T(4,128)(2,1)} %broadcast_in_dim.12), calls=%async_computation.1 | async-start | bytes 524288 | tf_op jit(solution)/shard_map/all_to_all | solution.py:349
  61.1 8.7 %collective-permute-start.14 = (bf16[768,128]{1,0:T(8,128)(2,1)}, bf16[768,128]{1,0:T(8,128)(2,1)S(1)}, u32[]{:S(2)}, u32[]{:S(2)}) collective-permute-start(bf16[768,128]{1,0:T(8,128)(2,1)} %get-tuple-element.59), channel_id=1, source_target_pairs={{0,3},{1,14},{2,5},{3,0},{4,7},{5,2},{6,9},{7,4},{8,11},{9,6},{10,... | collective-permute-start | bytes 589832 | tf_op jit(solution)/shard_map/ppermute | solution.py:345
  61.4 12.7 %collective-permute-start.2 = (bf16[768,128]{1,0:T(8,128)(2,1)}, bf16[768,128]{1,0:T(8,128)(2,1)S(1)}, u32[]{:S(2)}, u32[]{:S(2)}) collective-permute-start(bf16[768,128]{1,0:T(8,128)(2,1)} %get-tuple-element.46), channel_id=1, source_target_pairs={{0,15},{1,2},{2,1},{3,4},{4,3},{5,6},{6,5},{7,8},{8,7},{9,10},{10,... | collective-permute-start | bytes 589832 | tf_op jit(solution)/shard_map/ppermute | solution.py:345
  64.2 9.9 %collective-permute-start.3 = (bf16[768,128]{1,0:T(8,128)(2,1)}, bf16[768,128]{1,0:T(8,128)(2,1)S(1)}, u32[]{:S(2)}, u32[]{:S(2)}) collective-permute-start(bf16[768,128]{1,0:T(8,128)(2,1)} %get-tuple-element.47), channel_id=1, source_target_pairs={{0,1},{1,0},{2,3},{3,2},{4,5},{5,4},{6,7},{7,6},{8,9},{9,8},{10,11... | collective-permute-start | bytes 589832 | tf_op jit(solution)/shard_map/ppermute | solution.py:345
  64.2 10.9 %collective-permute-start = (bf16[768,128]{1,0:T(8,128)(2,1)}, bf16[768,128]{1,0:T(8,128)(2,1)S(1)}, u32[]{:S(2)}, u32[]{:S(2)}) collective-permute-start(bf16[768,128]{1,0:T(8,128)(2,1)} %get-tuple-element.44), channel_id=1, source_target_pairs={{0,10},{1,7},{2,12},{3,9},{4,14},{5,11},{6,0},{7,13},{8,2},{9,15},... | collective-permute-start | bytes 589832 | tf_op jit(solution)/shard_map/ppermute | solution.py:345
  65.7 17.6 %collective-permute-start.1 = (bf16[768,128]{1,0:T(8,128)(2,1)}, bf16[768,128]{1,0:T(8,128)(2,1)S(1)}, u32[]{:S(2)}, u32[]{:S(2)}) collective-permute-start(bf16[768,128]{1,0:T(8,128)(2,1)} %get-tuple-element.45), channel_id=1, source_target_pairs={{0,11},{1,6},{2,13},{3,8},{4,15},{5,10},{6,1},{7,12},{8,3},{9,14},... | collective-permute-start | bytes 589832 | tf_op jit(solution)/shard_map/ppermute | solution.py:345
  69.8 0.9 %copy-start = (bf16[768,128]{1,0:T(8,128)(2,1)S(1)}, bf16[768,128]{1,0:T(8,128)(2,1)}, u32[]{:S(2)}) copy-start(bf16[768,128]{1,0:T(8,128)(2,1)} %get-tuple-element.48.refs_1_) | copy-start | bytes 589828
